TPU v7x, 32 devices: a whole 2x2x4 slice. The times are simulated.
32 devices in a mesh: seq: 8 (over z, core), tp: 4 (over y, x).
Axes of the slice: x: 2, y: 2, z: 4, core: 2. Of those that a mesh axis runs over, the one named last changes fastest.
Arguments:
- tokens: bfloat16 [2048, 4608], P('seq', 'tp'), may hold values from -6 to 6
- attention_gain: float32 [4608], replicated, may hold values from 0.25 to 1.75
- query_weight: bfloat16 [4608, 4096], P(None, 'tp'), may hold values from -0.09375 to 0.09375
- key_weight: bfloat16 [4608, 2048], P(None, 'tp'), may hold values from -0.09375 to 0.09375
- value_weight: bfloat16 [4608, 2048], P(None, 'tp'), may hold values from -0.09375 to 0.09375
- output_weight: bfloat16 [4096, 4608], P('tp'), may hold values from -0.09375 to 0.09375
- post_gain: float32 [4608], replicated, may hold values from 0.25 to 1.75
- local_gain: float32 [4608], replicated, may hold values from 0.25 to 1.75
- local_query_weight: bfloat16 [4608, 4096], P(None, 'tp'), may hold values from -0.09375 to 0.09375
- local_key_weight: bfloat16 [4608, 2048], P(None, 'tp'), may hold values from -0.09375 to 0.09375
- local_value_weight: bfloat16 [4608, 2048], P(None, 'tp'), may hold values from -0.09375 to 0.09375
Outputs:
- hidden: bfloat16 [2048, 4608], P('seq', 'tp')
- local_heads: bfloat16 [2048, 4096], P('seq', 'tp')
All inputs are finite; a program needn't handle non-finite values.
Results may differ from a plain program's by a relative error of at most 0.02.
Values may be sent and summed in bfloat16 or wider, within the bound.
A program may use at most 128 MiB of HBM per device.

v0:
```python
import jax
import jax.numpy as jnp
from jax import lax
from jax.sharding import PartitionSpec as P

D = 4608
HEADS = 32
HEAD_DIM = 128
SOFT_CAP = 50.0
NORM_EPS = 1e-06


def passed_along(value, axis, steps):
    count = lax.axis_size(axis)
    leading, last = (max(0, -steps), min(count, count - steps))
    return lax.ppermute(value, axis, [(source, source + steps) for source in range(leading, last)])


def rms_scaled(values, weights):
    widened = values.astype(jnp.float32)
    factor = lax.rsqrt(jnp.mean(widened * widened, axis=-1, keepdims=True) + NORM_EPS)
    return widened * factor * weights


def rotate(vectors, places):
    head_size = vectors.shape[-1]
    halfway = head_size // 2
    exponents = jnp.arange(halfway, dtype=jnp.float32) * (2.0 / head_size)
    frequency = jnp.power(jnp.float32(10000.0), -exponents)
    angles = places.astype(jnp.float32)[:, None] * frequency[None, :]
    cosine_part = jnp.cos(angles)[:, None, :]
    sine_part = jnp.sin(angles)[:, None, :]
    first_half = vectors[..., :halfway]
    second_half = vectors[..., halfway:]
    return jnp.concatenate(
        [
            first_half * cosine_part - second_half * sine_part,
            second_half * cosine_part + first_half * sine_part,
        ],
        axis=-1,
    )


def project_heads(normed, weight_query, weight_key, weight_value, places):
    row_count = normed.shape[0]
    queries = jnp.dot(normed, weight_query, preferred_element_type=jnp.float32).reshape(
        row_count, -1, HEAD_DIM
    )
    key_heads = jnp.dot(normed, weight_key, preferred_element_type=jnp.float32).reshape(
        row_count, -1, HEAD_DIM
    )
    value_heads = jnp.dot(normed, weight_value, preferred_element_type=jnp.float32).reshape(
        row_count, -1, HEAD_DIM
    )
    return (
        rotate(queries, places).astype(jnp.bfloat16),
        rotate(key_heads, places).astype(jnp.bfloat16),
        value_heads.astype(jnp.bfloat16),
    )


def empty_carry(queries, kv_heads):
    row_count = queries.shape[0]
    groups = queries.shape[1] // kv_heads
    return (
        jnp.zeros((row_count, kv_heads, groups, HEAD_DIM), jnp.float32),
        jnp.zeros((kv_heads, groups, row_count), jnp.float32),
    )


def attend_block(queries, query_places, key_block, value_block, key_places, window_size):
    kv_heads = key_block.shape[1]
    groups = queries.shape[1] // kv_heads
    grouped = queries.reshape(queries.shape[0], kv_heads, groups, queries.shape[2])
    scale = float(D // HEADS) ** (-0.5)
    scores = (
        jnp.einsum("qhrd,khd->hrqk", grouped, key_block, preferred_element_type=jnp.float32) * scale
    )
    scores = SOFT_CAP * jnp.tanh(scores / SOFT_CAP)
    offset = query_places[:, None] - key_places[None, :]
    allowed = (offset >= 0) & (key_places >= 0)[None, :]
    if window_size is not None:
        allowed = allowed & (offset < window_size)
    weights = jnp.where(allowed[None, None], jnp.exp(scores), jnp.float32(0.0))
    denominator = jnp.sum(weights, axis=-1)
    numerator = jnp.einsum(
        "hrqk,khd->qhrd",
        weights.astype(jnp.bfloat16),
        value_block,
        preferred_element_type=jnp.float32,
    )
    return (numerator, denominator)


def finish_heads(running):
    numerator, denominator = running
    averaged = numerator / jnp.transpose(denominator, (2, 0, 1))[..., None]
    return averaged.astype(jnp.bfloat16).reshape(numerator.shape[0], -1)


def visit_one(partial_sum, query_set, key_block, value_block, key_places, needed):

    def compute(current):
        return attend_block(query_set[0], query_set[1], key_block, value_block, key_places, None)

    return lax.cond(needed, compute, lambda current: current, partial_sum)


def causal_sets(query_sets, key_heads, value_heads):
    kv_heads = key_heads.shape[1]
    initial = tuple((empty_carry(query_set[0], kv_heads) for query_set in query_sets))
    latest = tuple((jnp.max(query_set[1]) for query_set in query_sets))
    first_row = jnp.int32(0)
    key_block = lax.all_gather(key_heads, "seq", axis=0, tiled=True)
    value_block = lax.all_gather(value_heads, "seq", axis=0, tiled=True)
    key_places = lax.iota(jnp.int32, key_block.shape[0])
    updated = []
    for query_set, visit_partial_sum, newest in zip(query_sets, initial, latest):
        updated.append(
            visit_one(
                visit_partial_sum,
                query_set,
                key_block,
                value_block,
                key_places,
                first_row <= newest,
            )
        )
    totals = tuple(updated)
    return [finish_heads(partial_sum) for partial_sum in totals]


def local(
    tokens,
    attention_gain,
    query_weight,
    key_weight,
    value_weight,
    output_weight,
    post_gain,
    local_gain,
    local_query_weight,
    local_key_weight,
    local_value_weight,
):
    row_count = tokens.shape[0]
    column_count = tokens.shape[1]
    section_index = lax.axis_index("seq")
    places = section_index * row_count + lax.iota(jnp.int32, row_count)
    full_rows = lax.all_gather(tokens, "tp", axis=1, tiled=True)
    normed = rms_scaled(full_rows, attention_gain).astype(jnp.bfloat16)
    queries, key_heads, value_heads = project_heads(
        normed, query_weight, key_weight, value_weight, places
    )
    attended = causal_sets([(queries, places)], key_heads, value_heads)[0]
    summed = lax.psum(
        jnp.dot(attended, output_weight, preferred_element_type=jnp.float32).astype(jnp.bfloat16),
        "tp",
    ).astype(jnp.float32)
    whole_hidden = (full_rows.astype(jnp.float32) + rms_scaled(summed, post_gain)).astype(
        jnp.bfloat16
    )
    hidden = lax.dynamic_slice_in_dim(
        whole_hidden, lax.axis_index("tp") * column_count, column_count, 1
    )
    local_normed = rms_scaled(whole_hidden, local_gain).astype(jnp.bfloat16)
    local_queries, local_keys, local_values = project_heads(
        local_normed, local_query_weight, local_key_weight, local_value_weight, places
    )
    window_size = row_count // 2
    tails = jnp.stack(
        [local_keys[row_count - window_size :], local_values[row_count - window_size :]]
    )
    earlier = passed_along(tails, "seq", 1)
    key_block = jnp.concatenate([earlier[0], local_keys], axis=0)
    value_block = jnp.concatenate([earlier[1], local_values], axis=0)
    key_places = (
        section_index * row_count - window_size + lax.iota(jnp.int32, window_size + row_count)
    )
    result = attend_block(local_queries, places, key_block, value_block, key_places, window_size)
    local_heads = finish_heads(result)
    return (hidden, local_heads)


def solution(mesh):
    in_specs = (
        P("seq", "tp"),
        P(),
        P(None, "tp"),
        P(None, "tp"),
        P(None, "tp"),
        P("tp", None),
        P(),
        P(),
        P(None, "tp"),
        P(None, "tp"),
        P(None, "tp"),
    )
    out_specs = (P("seq", "tp"), P("seq", "tp"))
    return jax.shard_map(local, mesh=mesh, in_specs=in_specs, out_specs=out_specs, check_vma=False)
```

profile of v0, /device:TPU:1, one launch (start us, length us, event | category | flops | bytes accessed | tf_op | source)
XLA Modules:
  0.0 260.0 jit_solution(231217193242092318)
XLA Ops:
  9.2 39.9 %all-gather.4.cloned.1.call-done = bf16[256,4608]{1,0:T(8,128)(2,1)} async-done(((bf16[256,1152]{1,0:T(8,128)(2,1)}), bf16[256,4608]{1,0:T(8,128)(2,1)}) %all-gather.4.cloned.1.call-update) | async-done | bytes 2359312 | tf_op jit(solution)/shard_map/all_gather | solution.py:150
  49.1 2.2 fusion.22
  51.3 5.3 %fusion.58 = f32[256,512]{1,0:T(8,128)} fusion(bf16[4608,512]{1,0:T(8,128)(2,1)} %param.16, bf16[256,4608]{1,0:T(8,128)(2,1)} %all-gather.4.cloned.1.call-done, f32[4608]{0:T(1024)} %param.14, f32[256]{0:T(256)S(1)} %add_rsqrt_fusion.2), kind=kOutput, calls=%fused_computation.94 | convolution fusion | flops 1212678144 | bytes 7621632 | tf_op jit(solution)/shard_map/dot_general | solution.py:49
  56.6 1.4 reshape.222
  59.4 3.8 %fusion.34 = bf16[32,4,8,128]{3,2,1,0:T(8,128)(2,1)S(1)} fusion(bf16[4608,512]{1,0:T(8,128)(2,1)} %param.17, bf16[256,4608]{1,0:T(8,128)(2,1)S(1)} %copy-done, f32[4608]{0:T(1024)S(1)} %copy-done.15, f32[256]{0:T(256)S(1)} %add_rsqrt_fusion.2), kind=kOutput, calls=%fused_computation.42 | convolution fusion | flops 1212809216 | bytes 7359488 | tf_op jit(solution)/shard_map/dot_general | solution.py:52
  65.2 5.6 %convolution_bitcast_fusion.1 = f32[32,8,8,128]{3,1,2,0:T(8,128)S(1)} fusion(bf16[4608,1024]{1,0:T(8,128)(2,1)} %param.15, bf16[256,4608]{1,0:T(8,128)(2,1)S(1)} %copy-done, f32[4608]{0:T(1024)S(1)} %copy-done.15, f32[256]{0:T(256)S(1)} %add_rsqrt_fusion.2), kind=kOutput, calls=%fused_computation.38 | convolution fusion | flops 2420637696 | bytes 12864512 | tf_op jit(solution)/shard_map/dot_general | solution.py:46
  72.8 16.4 %all-gather.6.cloned.1.call-done = bf16[2048,4,128]{2,0,1:T(8,128)(2,1)} async-done(((bf16[256,4,128]{2,0,1:T(8,128)(2,1)}), bf16[2048,4,128]{2,0,1:T(8,128)(2,1)}) %all-gather.6.cloned.1.call-update) | async-done | bytes 2097168 | tf_op jit(solution)/shard_map/all_gather | solution.py:114
  89.2 30.2 %all-gather.8.cloned.1.call-done = bf16[2048,4,128]{2,0,1:T(8,128)(2,1)} async-done(((bf16[256,4,128]{2,0,1:T(8,128)(2,1)}), bf16[2048,4,128]{2,0,1:T(8,128)(2,1)}) %all-gather.8.cloned.1.call-update) | async-done | bytes 2097168 | tf_op jit(solution)/shard_map/all_gather | solution.py:115
  119.4 17.3 %conditional.1 = (f32[4,2,256]{2,1,0:T(2,128)S(1)}, f32[256,4,2,128]{0,3,2,1:T(8,128)S(1)}) conditional(s32[]{:T(128)} %convert_element_type.65, () %tuple.16, (s32[256]{0:T(256)}, s32[2048]{0:T(1024)S(1)}, s32[2048]{0:T(1024)S(1)}, bf16[256,8,128]{2,0,1:T(8,128)(2,1)}, bf16[2048,4,128]{2,0,1:T(8,128)(2,1)}, ...), branch_computations={%region_2.0_spmd, %region_3.5_spmd} | conditional | flops 2182610944 | bytes 51409964 | solution.py:106
  119.4 2.2 fusion.8
  121.6 6.8 %fusion = (f32[4,2,256]{2,1,0:T(2,128)S(1)}, f32[4,2048,256,2]{2,1,3,0:T(8,128)S(1)}) fusion(pred[256,2048]{0,1:T(8,128)(4,1)S(1)} %fusion.8, bf16[256,4,2,128]{3,0,2,1:T(8,128)(2,1)} %bitcast.90, bf16[2048,4,128]{2,0,1:T(8,128)(2,1)} %get-tuple-element.14), kind=kOutput, calls=%fused_computation.1 | convolution fusion | flops 1090516992 | bytes 19931136 | tf_op jit(solution)/shard_map/cond/branch_1_fun/qhrd,khd->hrqk/dot_general | solution.py:77
  128.4 6.5 %fusion.9 = f32[256,4,2,128]{3,0,2,1:T(8,128)} fusion(bf16[2048,4,128]{2,0,1:T(8,128)(2,1)S(1)} %copy-done.14, f32[4,2048,256,2]{2,1,3,0:T(8,128)S(1)} %get-tuple-element.31, pred[256,2048]{0,1:T(8,128)(4,1)S(1)} %fusion.8), kind=kOutput, calls=%fused_computation.10 | convolution fusion | flops 1090519040 | bytes 20447232 | tf_op jit(solution)/shard_map/cond/branch_1_fun/hrqk,khd->qhrd/dot_general | solution.py:86
  134.9 1.6 copy.52
  136.8 7.6 %convolution_convert_fusion = bf16[256,4608]{1,0:T(8,128)(2,1)} fusion(bf16[256,1024]{0,1:T(8,128)(2,1)S(1)} %bitcast.88, bf16[1024,4608]{1,0:T(8,128)(2,1)} %param.18), kind=kOutput, calls=%fused_computation.18 | convolution fusion | flops 2417098752 | bytes 12320768 | tf_op jit(solution)/shard_map/dot_general | solution.py:157
  145.4 71.9 %all-reduce.2.cloned.1.call-done = bf16[256,4608]{1,0:T(8,128)(2,1)} async-done(((bf16[256,4608]{1,0:T(8,128)(2,1)}), bf16[256,4608]{1,0:T(8,128)(2,1)}) %all-reduce.2.cloned.1.call-update) | async-done | bytes 2359312 | tf_op jit(solution)/shard_map/psum | solution.py:156
  217.3 2.2 fusion.17
  219.6 3.2 %fusion.19 = (f32[256]{0:T(256)S(1)}, bf16[256,4608]{1,0:T(8,128)(2,1)S(1)}) fusion(f32[4608]{0:T(1024)S(1)} %copy-done.12, f32[256]{0:T(256)S(1)} %add_rsqrt_fusion.1, bf16[256,4608]{1,0:T(8,128)(2,1)} %all-reduce.2.cloned.1.call-done, bf16[256,4608]{1,0:T(8,128)(2,1)S(1)} %copy-done), kind=kLoop, calls=%fused_computation.25 | loop fusion | flops 10616576 | bytes 7098368 | tf_op jit(solution)/shard_map/reduce_sum | solution.py:21
  222.8 6.1 %convolution_bitcast_fusion = f32[32,8,8,128]{3,1,2,0:T(8,128)S(1)} fusion(bf16[4608,1024]{1,0:T(8,128)(2,1)} %param.21, bf16[256,4608]{1,0:T(8,128)(2,1)S(1)} %get-tuple-element.29, f32[4608]{0:T(1024)S(1)} %copy-done.16, f32[256]{0:T(256)S(1)} %add_rsqrt_fusion), kind=kOutput, calls=%fused_computation.37 | convolution fusion | flops 2420637696 | bytes 12864512 | tf_op jit(solution)/shard_map/dot_general | solution.py:46
  229.6 1.4 fusion.63
  232.3 4.5 %convolution_convert_fusion.1 = bf16[256,512]{1,0:T(8,128)(2,1)S(1)} fusion(bf16[4608,512]{1,0:T(8,128)(2,1)} %param.23, bf16[256,4608]{1,0:T(8,128)(2,1)} %copy-done.1, f32[4608]{0:T(1024)S(1)} %copy-done.17, f32[256]{0:T(256)S(1)} %add_rsqrt_fusion), kind=kOutput, calls=%fused_computation.40 | convolution fusion | flops 1212809216 | bytes 7359488 | tf_op jit(solution)/shard_map/dot_general | solution.py:52
  241.0 4.0 %collective-permute-start = (bf16[2,128,4,128]{3,1,2,0:T(8,128)(2,1)}, bf16[2,128,4,128]{3,1,2,0:T(8,128)(2,1)S(1)}, u32[]{:S(2)}, u32[]{:S(2)}) collective-permute-start(bf16[2,128,4,128]{3,1,2,0:T(8,128)(2,1)} %pad_maximum_fusion.2), channel_id=1, source_target_pairs={{0,4},{4,8},{8,12},{12,16},{16,20},{20,24},{24,28},{1,5},{5,9},{9,... | collective-permute-start | bytes 786440 | tf_op jit(solution)/shard_map/ppermute | solution.py:16
  245.0 1.4 subtract_convert_fusion
  246.5 1.9 constant_dynamic-slice_fusion
  248.8 2.6 fusion.26
  (86 shorter events, 16.3 us)
Async XLA Ops:
  7.2 41.9 %all-gather.4.cloned.1.call-start = ((), (), s32[]{:S(2)}) async-start(), calls=%async_computation | async-start | bytes 2949120 | tf_op jit(solution)/shard_map/all_gather | solution.py:150
  7.9 81.3 %all-gather.6.cloned.1.call-start = ((), (), s32[]{:S(2)}) async-start(), calls=%async_computation.1 | async-start | bytes 2359296 | tf_op jit(solution)/shard_map/all_gather | solution.py:114
  9.2 62.1 %copy-start.2 = (f32[256,64]{1,0:T(8,128)}, f32[256,64]{1,0:T(8,128)S(1)}, u32[]{:S(2)}) copy-start(f32[256,64]{1,0:T(8,128)S(1)} %get-tuple-element.51) | copy-start | bytes 196612
  56.6 2.8 %copy-start = (bf16[256,4608]{1,0:T(8,128)(2,1)S(1)}, bf16[256,4608]{1,0:T(8,128)(2,1)}, u32[]{:S(2)}) copy-start(bf16[256,4608]{1,0:T(8,128)(2,1)} %all-gather.4.cloned.1.call-done) | copy-start | bytes 7077892
  56.6 2.8 %copy-start.15 = (f32[4608]{0:T(1024)S(1)}, f32[4608]{0:T(1024)}, u32[]{:S(2)}) copy-start(f32[4608]{0:T(1024)} %param.14) | copy-start | bytes 55300
  59.3 60.1 %all-gather.8.cloned.1.call-start = ((), (), s32[]{:S(2)}) async-start(), calls=%async_computation.2 | async-start | bytes 2359296 | tf_op jit(solution)/shard_map/all_gather | solution.py:115
  64.0 153.3 %all-reduce.2.cloned.1.call-start = ((), (), s32[]{:S(2)}) async-start(), calls=%async_computation.3 | async-start | bytes 4718592 | tf_op jit(solution)/shard_map/psum | solution.py:156
  121.6 6.8 %copy-start.14 = (bf16[2048,4,128]{2,0,1:T(8,128)(2,1)S(1)}, bf16[2048,4,128]{2,0,1:T(8,128)(2,1)}, u32[]{:S(2)}) copy-start(bf16[2048,4,128]{2,0,1:T(8,128)(2,1)} %get-tuple-element.16) | copy-start | bytes 6291460 | tf_op jit(solution)/shard_map/cond
  136.8 7.7 %copy-start.13 = (s32[256]{0:T(256)S(1)}, s32[256]{0:T(256)}, u32[]{:S(2)}) copy-start(s32[256]{0:T(256)} %iota_add_fusion.1) | copy-start | bytes 3076
  144.4 75.1 %copy-start.12 = (f32[4608]{0:T(1024)S(1)}, f32[4608]{0:T(1024)}, u32[]{:S(2)}) copy-start(f32[4608]{0:T(1024)} %param.19) | copy-start | bytes 55300
  145.4 77.4 %copy-start.16 = (f32[4608]{0:T(1024)S(1)}, f32[4608]{0:T(1024)}, u32[]{:S(2)}) copy-start(f32[4608]{0:T(1024)} %param.20) | copy-start | bytes 55300
  219.5 10.0 %slice-start = ((s8[4718592]{0:T(1024)(128)(4,1)}), s8[4194304]{0:T(1024)(128)(4,1)S(1)}, s32[]{:S(2)}) async-start(s8[4718592]{0:T(1024)(128)(4,1)} %bitcast.96), calls=%async_computation.4 | async-start | bytes 8388608
  222.8 6.7 %copy-start.1 = (bf16[256,4608]{1,0:T(8,128)(2,1)}, bf16[256,4608]{1,0:T(8,128)(2,1)S(1)}, u32[]{:S(2)}) copy-start(bf16[256,4608]{1,0:T(8,128)(2,1)S(1)} %get-tuple-element.29) | copy-start | bytes 7077892
  222.8 6.7 %slice-start.1 = ((s8[4718592]{0:T(1024)(128)(4,1)}), s8[524288]{0:T(1024)(128)(4,1)S(1)}, s32[]{:S(2)}) async-start(s8[4718592]{0:T(1024)(128)(4,1)} %bitcast.96), calls=%async_computation.5 | async-start | bytes 1048576
  229.6 2.8 %copy-start.17 = (f32[4608]{0:T(1024)S(1)}, f32[4608]{0:T(1024)}, u32[]{:S(2)}) copy-start(f32[4608]{0:T(1024)} %param.20) | copy-start | bytes 55300
  232.3 6.9 %copy-start.3 = (f32[256,64]{1,0:T(8,128)S(1)}, f32[256,64]{1,0:T(8,128)}, u32[]{:S(2)}) copy-start(f32[256,64]{1,0:T(8,128)} %copy-done.2) | copy-start | bytes 196612
  232.3 6.9 %copy-start.4 = (f32[256,4,64]{2,1,0:T(4,128)S(1)}, f32[256,4,64]{2,1,0:T(4,128)}, u32[]{:S(2)}) copy-start(f32[256,4,64]{2,1,0:T(4,128)} %get-tuple-element.45) | copy-start | bytes 786436
  236.9 0.7 copy-start.9
  239.4 0.8 copy-start.7
  239.4 7.0 %copy-start.10 = (bf16[256,512]{1,0:T(8,128)(2,1)S(1)}, bf16[256,512]{1,0:T(8,128)(2,1)}, u32[]{:S(2)}) copy-start(bf16[256,512]{1,0:T(8,128)(2,1)} %copy-done.9) | copy-start | bytes 786436
  240.2 8.5 %copy-start.6 = (bf16[256,4,64]{2,0,1:T(8,128)(2,1)S(1)}, bf16[256,4,64]{2,0,1:T(8,128)(2,1)}, u32[]{:S(2)}) copy-start(bf16[256,4,64]{2,0,1:T(8,128)(2,1)} %copy-done.5) | copy-start | bytes 393220
  241.0 7.8 %copy-start.8 = (bf16[256,4,64]{2,0,1:T(8,128)(2,1)S(1)}, bf16[256,4,64]{2,0,1:T(8,128)(2,1)}, u32[]{:S(2)}) copy-start(bf16[256,4,64]{2,0,1:T(8,128)(2,1)} %copy-done.7) | copy-start | bytes 393220
  241.0 7.8 %copy-start.11 = (pred[256,384]{0,1:T(8,128)(4,1)S(1)}, pred[256,384]{0,1:T(8,128)(4,1)}, u32[]{:S(2)}) copy-start(pred[256,384]{0,1:T(8,128)(4,1)} %fusion.48) | copy-start | bytes 294916
  241.0 7.6 %collective-permute-start = (bf16[2,128,4,128]{3,1,2,0:T(8,128)(2,1)}, bf16[2,128,4,128]{3,1,2,0:T(8,128)(2,1)S(1)}, u32[]{:S(2)}, u32[]{:S(2)}) collective-permute-start(bf16[2,128,4,128]{3,1,2,0:T(8,128)(2,1)} %pad_maximum_fusion.2), channel_id=1, source_target_pairs={{0,4},{4,8},{8,12},{12,16},{16,20},{20,24},{24,28},{1,5},{5,9},{9,... | collective-permute-start | bytes 786440 | tf_op jit(solution)/shard_map/ppermute | solution.py:16
  (1 other events, 0.7 us)
Sparse Core Ops, SparseCore 0:
  9.8 39.2 all-gather.3
  59.5 29.7 all-gather.5
  90.8 28.5 all-gather.7
  144.6 72.6 all-reduce.1
where the time goes:
time: 260 us
  waiting for transfers between devices  159 us (61%)
  matrix products  51.3 us (20%)
  other arithmetic  17.5 us (7%)
  between operations  14.8 us (6%)
  local copies, waits for them, and re-layouts  12.7 us (5%)
  starting transfers between devices  4.14 us (2%)
    psum x1, waiting for transfers between devices, local(): lax.psum(jnp.dot(attended, output_weight, preferred_element_type=jnp.floa...  71.9 us
    all_gather x1, waiting for transfers between devices, local(): full_rows = lax.all_gather(tokens, 'tp', axis=1, tiled=True)  39.9 us
    all_gather x1, waiting for transfers between devices, causal_sets(): value_block = lax.all_gather(value_heads, 'seq', axis=0, tiled=True)  30.2 us
    all_gather x1, waiting for transfers between devices, causal_sets(): key_block = lax.all_gather(key_heads, 'seq', axis=0, tiled=True)  16.4 us
    dot_general x2, matrix products, project_heads(): jnp.dot(normed, weight_query, preferred_element_type=jnp.float32)  11.7 us
    dot_general x2, matrix products, attend_block(): jnp.einsum('qhrd,khd->hrqk', grouped, key_block, preferred_element_type=j...  9.32 us
    dot_general x2, matrix products, project_heads(): jnp.dot(normed, weight_value, preferred_element_type=jnp.float32)  8.31 us
    dot_general x2, matrix products, attend_block(): jnp.einsum('hrqk,khd->qhrd', weights.astype(jnp.bfloat16), value_block, p...  7.66 us
  transfers between devices with their start and end apart: 5, of which 5 were waited for; matrix products, arithmetic and copies ran while one was open for 7% of the time, Pallas kernels for 0%

commit v1 on v0

--- a/solution.py
+++ b/solution.py
@@ -8,6 +8,12 @@
 HEAD_DIM = 128
 SOFT_CAP = 50.0
 NORM_EPS = 1e-06
+
+
+def add_all(shard, axis):
+    shards = lax.all_gather(shard, axis, axis=0, tiled=False)
+    total = shards.sum(axis=0)
+    return total
 
 
 def passed_along(value, axis, steps):
@@ -153,7 +159,7 @@
         normed, query_weight, key_weight, value_weight, places
     )
     attended = causal_sets([(queries, places)], key_heads, value_heads)[0]
-    summed = lax.psum(
+    summed = add_all(
         jnp.dot(attended, output_weight, preferred_element_type=jnp.float32).astype(jnp.bfloat16),
         "tp",
     ).astype(jnp.float32)

time: 260 us -> 287 us (1.10)
  waiting for transfers between devices: 159 us -> 184 us
  other arithmetic: 17.5 us -> 20.6 us
    all_gather x0 -> x1, waiting for transfers between devices: none -> 95 us  [add_all(): shards = lax.all_gather(shard, axis, axis=0, tiled=False)]
    psum x1 -> x0, waiting for transfers between devices: 71.9 us -> none  [local(): lax.psum(jnp.dot(attended, output_weight, preferred_element_type=jnp.floa...]
    reduce_sum x0 -> x1, other arithmetic: none -> 6.49 us  [add_all(): total = shards.sum(axis=0)]
  transfers between devices with their start and end apart: 5 -> 5, of which waited for: 5 -> 4; matrix products, arithmetic and copies ran while one was open for 7% -> 6% of each run, Pallas kernels for 0% -> 0%
where the time goes in v1:
time: 287 us; the launch traced here: 286 us
  waiting for transfers between devices  184 us (64%)
  matrix products  51 us (18%)
  other arithmetic  20.6 us (7%)
  between operations  14.8 us (5%)
  local copies, waits for them, and re-layouts  11.2 us (4%)
  starting transfers between devices  4.23 us (1%)
    all_gather x1, waiting for transfers between devices, add_all(): shards = lax.all_gather(shard, axis, axis=0, tiled=False)  95 us
    all_gather x1, waiting for transfers between devices, local(): full_rows = lax.all_gather(tokens, 'tp', axis=1, tiled=True)  39.9 us
    all_gather x1, waiting for transfers between devices, causal_sets(): value_block = lax.all_gather(value_heads, 'seq', axis=0, tiled=True)  30.8 us
    all_gather x1, waiting for transfers between devices, causal_sets(): key_block = lax.all_gather(key_heads, 'seq', axis=0, tiled=True)  17.8 us
    dot_general x2, matrix products, project_heads(): jnp.dot(normed, weight_query, preferred_element_type=jnp.float32)  11.6 us
    dot_general x2, matrix products, attend_block(): jnp.einsum('qhrd,khd->hrqk', grouped, key_block, preferred_element_type=j...  9.16 us
    dot_general x2, matrix products, project_heads(): jnp.dot(normed, weight_value, preferred_element_type=jnp.float32)  8.3 us
    dot_general x1, matrix products, local(): jnp.dot(attended, output_weight, preferred_element_type=jnp.float32)  7.6 us
  transfers between devices with their start and end apart: 5, of which 4 were waited for; matrix products, arithmetic and copies ran while one was open for 6% of the time, Pallas kernels for 0%

profile of v1, /device:TPU:1, one launch (start us, length us, event | category | flops | bytes accessed | tf_op | source)
XLA Modules:
  0.0 286.3 jit_solution(17981664426763814852)
XLA Ops:
  9.2 39.9 %all-gather.6.cloned.1.call-done = bf16[256,4608]{1,0:T(8,128)(2,1)} async-done(((bf16[256,1152]{1,0:T(8,128)(2,1)}), bf16[256,4608]{1,0:T(8,128)(2,1)}) %all-gather.6.cloned.1.call-update) | async-done | bytes 2359312 | tf_op jit(solution)/shard_map/all_gather | solution.py:156
  49.1 2.2 fusion.22
  51.3 5.3 %fusion.58 = f32[256,512]{1,0:T(8,128)} fusion(bf16[4608,512]{1,0:T(8,128)(2,1)} %param.16, bf16[256,4608]{1,0:T(8,128)(2,1)} %all-gather.6.cloned.1.call-done, f32[4608]{0:T(1024)} %param.14, f32[256]{0:T(256)S(1)} %add_rsqrt_fusion.2), kind=kOutput, calls=%fused_computation.94 | convolution fusion | flops 1212678144 | bytes 7621632 | tf_op jit(solution)/shard_map/dot_general | solution.py:55
  56.6 1.4 reshape.222
  59.4 3.8 %fusion.34 = bf16[32,4,8,128]{3,2,1,0:T(8,128)(2,1)S(1)} fusion(bf16[4608,512]{1,0:T(8,128)(2,1)} %param.17, bf16[256,4608]{1,0:T(8,128)(2,1)S(1)} %copy-done, f32[4608]{0:T(1024)S(1)} %copy-done.7, f32[256]{0:T(256)S(1)} %add_rsqrt_fusion.2), kind=kOutput, calls=%fused_computation.42 | convolution fusion | flops 1212809216 | bytes 7359488 | tf_op jit(solution)/shard_map/dot_general | solution.py:58
  64.7 5.5 %convolution_bitcast_fusion.1 = f32[32,8,8,128]{3,1,2,0:T(8,128)S(1)} fusion(bf16[4608,1024]{1,0:T(8,128)(2,1)} %param.15, bf16[256,4608]{1,0:T(8,128)(2,1)S(1)} %copy-done, f32[4608]{0:T(1024)S(1)} %copy-done.7, f32[256]{0:T(256)S(1)} %add_rsqrt_fusion.2), kind=kOutput, calls=%fused_computation.38 | convolution fusion | flops 2420637696 | bytes 12864512 | tf_op jit(solution)/shard_map/dot_general | solution.py:52
  71.4 17.8 %all-gather.8.cloned.1.call-done = bf16[2048,4,128]{2,0,1:T(8,128)(2,1)} async-done(((bf16[256,4,128]{2,0,1:T(8,128)(2,1)}), bf16[2048,4,128]{2,0,1:T(8,128)(2,1)}) %all-gather.8.cloned.1.call-update) | async-done | bytes 2097168 | tf_op jit(solution)/shard_map/all_gather | solution.py:120
  89.2 30.8 %all-gather.10.cloned.1.call-done = bf16[2048,4,128]{2,0,1:T(8,128)(2,1)} async-done(((bf16[256,4,128]{2,0,1:T(8,128)(2,1)}), bf16[2048,4,128]{2,0,1:T(8,128)(2,1)}) %all-gather.10.cloned.1.call-update) | async-done | bytes 2097168 | tf_op jit(solution)/shard_map/all_gather | solution.py:121
  120.0 14.4 %conditional.1 = (f32[4,2,256]{2,1,0:T(2,128)S(1)}, f32[256,4,2,128]{0,3,2,1:T(8,128)S(1)}) conditional(s32[]{:T(128)} %convert_element_type.67, () %tuple.16, (s32[256]{0:T(256)S(1)}, s32[2048]{0:T(1024)S(1)}, s32[2048]{0:T(1024)S(1)}, bf16[256,8,128]{2,0,1:T(8,128)(2,1)S(1)}, bf16[2048,4,128]{2,0,1:T(8,128)(2,1)}, ...), branch_computations={%region_2.0_spmd, %region_3.5_spmd} | conditional | flops 2182610944 | bytes 51409964 | solution.py:112
  120.0 1.5 fusion.8
  121.5 6.6 %fusion = (f32[4,2,256]{2,1,0:T(2,128)S(1)}, f32[4,2048,256,2]{2,1,3,0:T(8,128)S(1)}) fusion(pred[256,2048]{0,1:T(8,128)(4,1)S(1)} %fusion.8, bf16[256,4,2,128]{3,0,2,1:T(8,128)(2,1)S(1)} %bitcast.92, bf16[2048,4,128]{2,0,1:T(8,128)(2,1)} %get-tuple-element.14), kind=kOutput, calls=%fused_computation.1 | convolution fusion | flops 1090516992 | bytes 19931136 | tf_op jit(solution)/shard_map/cond/branch_1_fun/qhrd,khd->hrqk/dot_general | solution.py:83
  128.1 5.7 %fusion.9 = f32[256,4,2,128]{3,0,2,1:T(8,128)S(1)} fusion(bf16[2048,4,128]{2,0,1:T(8,128)(2,1)S(1)} %copy-done.6, f32[4,2048,256,2]{2,1,3,0:T(8,128)S(1)} %get-tuple-element.31, pred[256,2048]{0,1:T(8,128)(4,1)S(1)} %fusion.8), kind=kOutput, calls=%fused_computation.10 | convolution fusion | flops 1090519040 | bytes 20447232 | tf_op jit(solution)/shard_map/cond/branch_1_fun/hrqk,khd->qhrd/dot_general | solution.py:92
  134.5 7.6 %convolution_convert_fusion = bf16[256,4608]{1,0:T(8,128)(2,1)} fusion(bf16[256,1024]{0,1:T(8,128)(2,1)S(1)} %bitcast.90, bf16[1024,4608]{1,0:T(8,128)(2,1)} %param.18), kind=kOutput, calls=%fused_computation.18 | convolution fusion | flops 2417098752 | bytes 12320768 | tf_op jit(solution)/shard_map/dot_general | solution.py:163
  142.3 95.0 %all-gather.12.cloned.1.call-done = bf16[1024,4608]{1,0:T(8,128)(2,1)} async-done(((bf16[256,4608]{1,0:T(8,128)(2,1)}), bf16[1024,4608]{1,0:T(8,128)(2,1)}) %all-gather.12.cloned.1.call-update) | async-done | bytes 9437200 | tf_op jit(solution)/shard_map/all_gather | solution.py:14
  237.3 6.5 %reduce_sum.58 = bf16[256,4608]{1,0:T(8,128)(2,1)S(1)} reduce(bf16[4,256,4608]{2,1,0:T(8,128)(2,1)} %bitcast.87, bf16[]{:T(256)} %constant.53.clone.1), dimensions={0}, to_apply=%region_5.6 | reduce | flops 3538944 | bytes 11796482 | tf_op jit(solution)/shard_map/reduce_sum | solution.py:15
  244.4 3.2 %fusion.19 = (f32[256]{0:T(256)S(1)}, bf16[256,4608]{1,0:T(8,128)(2,1)S(1)}) fusion(f32[4608]{0:T(1024)S(1)} %copy-done.5, f32[256]{0:T(256)S(1)} %add_rsqrt_fusion.1, bf16[256,4608]{1,0:T(8,128)(2,1)S(1)} %reduce_sum.58, bf16[256,4608]{1,0:T(8,128)(2,1)} %all-gather.6.cloned.1.call-done), kind=kLoop, calls=%fused_computation.25 | loop fusion | flops 10616576 | bytes 7098368 | tf_op jit(solution)/shard_map/reduce_sum | solution.py:27
  247.7 6.1 %convolution_bitcast_fusion = f32[32,8,8,128]{3,1,2,0:T(8,128)S(1)} fusion(bf16[4608,1024]{1,0:T(8,128)(2,1)} %param.21, bf16[256,4608]{1,0:T(8,128)(2,1)S(1)} %get-tuple-element.29, f32[4608]{0:T(1024)S(1)} %copy-done.8, f32[256]{0:T(256)S(1)} %add_rsqrt_fusion), kind=kOutput, calls=%fused_computation.37 | convolution fusion | flops 2420637696 | bytes 12864512 | tf_op jit(solution)/shard_map/dot_general | solution.py:52
  254.4 2.2 fusion.63
  257.8 1.3 fusion.68
  259.1 4.5 %convolution_convert_fusion.1 = bf16[256,512]{1,0:T(8,128)(2,1)S(1)} fusion(bf16[4608,512]{1,0:T(8,128)(2,1)} %param.23, bf16[256,4608]{1,0:T(8,128)(2,1)} %copy-done.1, f32[4608]{0:T(1024)S(1)} %copy-done.8, f32[256]{0:T(256)S(1)} %add_rsqrt_fusion), kind=kOutput, calls=%fused_computation.40 | convolution fusion | flops 1212809216 | bytes 7359488 | tf_op jit(solution)/shard_map/dot_general | solution.py:58
  266.4 4.1 %collective-permute-start = (bf16[2,128,4,128]{3,1,2,0:T(8,128)(2,1)}, bf16[2,128,4,128]{3,1,2,0:T(8,128)(2,1)}, u32[]{:S(2)}, u32[]{:S(2)}) collective-permute-start(bf16[2,128,4,128]{3,1,2,0:T(8,128)(2,1)} %pad_maximum_fusion.2), channel_id=1, source_target_pairs={{0,4},{4,8},{8,12},{12,16},{16,20},{20,24},{24,28},{1,5},{5,9},{9,... | collective-permute-start | bytes 786440 | tf_op jit(solution)/shard_map/ppermute | solution.py:22
  270.4 1.4 subtract_convert_fusion
  272.0 1.9 constant_dynamic-slice_fusion
  275.0 2.6 fusion.26
  (69 shorter events, 14.5 us)
Async XLA Ops:
  7.2 41.9 %all-gather.6.cloned.1.call-start = ((), (), s32[]{:S(2)}) async-start(), calls=%async_computation | async-start | bytes 2949120 | tf_op jit(solution)/shard_map/all_gather | solution.py:156
  7.9 81.3 %all-gather.8.cloned.1.call-start = ((), (), s32[]{:S(2)}) async-start(), calls=%async_computation.1 | async-start | bytes 2359296 | tf_op jit(solution)/shard_map/all_gather | solution.py:120
  56.6 2.8 copy-start
  56.6 2.8 copy-start.7
  59.3 60.7 %all-gather.10.cloned.1.call-start = ((), (), s32[]{:S(2)}) async-start(), calls=%async_computation.2 | async-start | bytes 2359296 | tf_op jit(solution)/shard_map/all_gather | solution.py:121
  64.0 173.4 %all-gather.12.cloned.1.call-start = ((), (), s32[]{:S(2)}) async-start(), calls=%async_computation.3 | async-start | bytes 11796480 | tf_op jit(solution)/shard_map/all_gather | solution.py:14
  121.5 6.6 %copy-start.6 = (bf16[2048,4,128]{2,0,1:T(8,128)(2,1)S(1)}, bf16[2048,4,128]{2,0,1:T(8,128)(2,1)}, u32[]{:S(2)}) copy-start(bf16[2048,4,128]{2,0,1:T(8,128)(2,1)} %get-tuple-element.16) | copy-start | bytes 6291460 | tf_op jit(solution)/shard_map/cond
  237.3 7.1 %copy-start.5 = (f32[4608]{0:T(1024)S(1)}, f32[4608]{0:T(1024)}, u32[]{:S(2)}) copy-start(f32[4608]{0:T(1024)} %param.19) | copy-start | bytes 55300
  243.8 3.8 %copy-start.8 = (f32[4608]{0:T(1024)S(1)}, f32[4608]{0:T(1024)}, u32[]{:S(2)}) copy-start(f32[4608]{0:T(1024)} %param.20) | copy-start | bytes 55300
  244.4 10.0 %slice-start = ((s8[4718592]{0:T(1024)(128)(4,1)}), s8[4194304]{0:T(1024)(128)(4,1)S(1)}, s32[]{:S(2)}) async-start(s8[4718592]{0:T(1024)(128)(4,1)} %bitcast.98), calls=%async_computation.4 | async-start | bytes 8388608
  247.6 6.7 %copy-start.1 = (bf16[256,4608]{1,0:T(8,128)(2,1)}, bf16[256,4608]{1,0:T(8,128)(2,1)S(1)}, u32[]{:S(2)}) copy-start(bf16[256,4608]{1,0:T(8,128)(2,1)S(1)} %get-tuple-element.29) | copy-start | bytes 7077892
  247.7 6.7 %slice-start.1 = ((s8[4718592]{0:T(1024)(128)(4,1)}), s8[524288]{0:T(1024)(128)(4,1)S(1)}, s32[]{:S(2)}) async-start(s8[4718592]{0:T(1024)(128)(4,1)} %bitcast.98), calls=%async_computation.5 | async-start | bytes 1048576
  259.1 5.2 %copy-start.2 = (f32[256,4,64]{2,1,0:T(4,128)S(1)}, f32[256,4,64]{2,1,0:T(4,128)}, u32[]{:S(2)}) copy-start(f32[256,4,64]{2,1,0:T(4,128)} %get-tuple-element.44) | copy-start | bytes 786436
  263.6 0.7 copy-start.3
  265.5 6.3 %copy-start.4 = (bf16[256,512]{1,0:T(8,128)(2,1)S(1)}, bf16[256,512]{1,0:T(8,128)(2,1)}, u32[]{:S(2)}) copy-start(bf16[256,512]{1,0:T(8,128)(2,1)} %copy-done.3) | copy-start | bytes 786436
  266.4 7.5 %collective-permute-start = (bf16[2,128,4,128]{3,1,2,0:T(8,128)(2,1)}, bf16[2,128,4,128]{3,1,2,0:T(8,128)(2,1)}, u32[]{:S(2)}, u32[]{:S(2)}) collective-permute-start(bf16[2,128,4,128]{3,1,2,0:T(8,128)(2,1)} %pad_maximum_fusion.2), channel_id=1, source_target_pairs={{0,4},{4,8},{8,12},{12,16},{16,20},{20,24},{24,28},{1,5},{5,9},{9,... | collective-permute-start | bytes 786440 | tf_op jit(solution)/shard_map/ppermute | solution.py:22
Sparse Core Ops, SparseCore 0:
  9.8 39.2 all-gather.5
  59.5 29.7 all-gather.7
  91.4 28.5 all-gather.9
  142.2 95.0 all-gather.11
